TPU v7x, 32 devices: a whole 2x2x4 slice. The times are simulated.
32 devices in a mesh: section: 4 (over y, core), dp: 2 (over x), expert: 4 (over z).
Axes of the slice: x: 2, y: 2, z: 4, core: 2. Of those that a mesh axis runs over, the one named last changes fastest.
Arguments:
- inputs: bfloat16 [4, 1024, 2048], P('section', ('dp', 'expert')), may hold values from -6 to 6
- in_cache: bfloat16 [4, 1024, 2048], P('section', ('dp', 'expert')), may hold values from -6 to 6
- out_cache: bfloat16 [4, 1024, 2048], P('section', ('dp', 'expert')), may hold values from -6 to 6
- w_up: bfloat16 [4, 2048, 57344], P('section', None, ('dp', 'expert')), may hold values from -0.125 to 0.125
- w_down: bfloat16 [4, 57344, 2048], P('section', ('dp', 'expert')), may hold values from -0.0625 to 0.0625
- routing: int32 [4, 1024, 2], P('section', ('dp', 'expert')), may hold values from 0 to 7, all different within a row; in each aligned block of 128 rows (0 to 127, 128 to 255, ..., all dimensions but the last counted through in order) at most 32 rows name the same one
- gate_table: int32 [4, 1024, 2], P('section', ('dp', 'expert')), may hold values from 1 to 16
- lengths: int32 [64], P(('dp', 'expert')), may hold values from 1 to 16
- sample_map: int32 [64], replicated, may hold values from 0 to 63, as said below
Outputs:
- next_input: bfloat16 [4, 1024, 2048], P('section', ('dp', 'expert'))
- new_out_cache: bfloat16 [4, 1024, 2048], P('section', ('dp', 'expert'))
Inputs may be any that keep to these rules, and one draw needn't show every extreme that they name: `sample_map`: A permutation. Every sample keeps its index along expert; the samples of one device go to exactly 2 replicas, exactly 4 to each. `routing`: A row names 2 different experts; in the rows of one device each expert is named exactly 32 times.
All inputs are finite; a program needn't handle non-finite values.
Results may differ from a plain program's by a relative error of at most 0.007.
Values may be sent and summed in bfloat16 or wider, within the bound.
A program may use at most 128 MiB of HBM per device.

v0:
```python
import jax
import jax.numpy as jnp
from jax import lax
from jax.sharding import PartitionSpec as P

EXPERTS = 8
TOPK = 2
ROWS = 16
SAMP_DEV = 8


def from_behind(value, axis, by):
    peers = lax.axis_size(axis)
    pairs = [(i, i + by) for i in range(peers) if 0 <= i + by < peers]
    return lax.ppermute(value, axis, pairs)


def per_device(inputs, in_cache, out_cache, w_up, w_down, routing, gate_table, lengths, sample_map):
    tok_rows = inputs.shape[1]
    feature_width = inputs.shape[2]
    dp_count = lax.axis_size("dp")
    expert_count = lax.axis_size("expert")
    group_size = dp_count * expert_count
    slice_count = group_size // EXPERTS
    own_dp = lax.axis_index("dp")
    own_device = own_dp * expert_count + lax.axis_index("expert")
    cap_slots = max(1, SAMP_DEV // dp_count)
    sample_ids = jnp.arange(SAMP_DEV, dtype=jnp.int32)
    own_map = lax.dynamic_slice_in_dim(sample_map, own_device * SAMP_DEV, SAMP_DEV)
    dest_dp = own_map // SAMP_DEV // expert_count
    onehot_dest = (dest_dp[:, None] == jnp.arange(dp_count, dtype=jnp.int32)[None, :]).astype(
        jnp.int32
    )
    slot_index = (jnp.cumsum(onehot_dest, axis=0) - onehot_dest)[sample_ids, dest_dp]
    empty_slots = jnp.zeros((dp_count, cap_slots, ROWS, feature_width), jnp.bfloat16)
    send_in = empty_slots.at[dest_dp, slot_index].set(
        in_cache[0].reshape(SAMP_DEV, ROWS, feature_width)
    )
    send_out = empty_slots.at[dest_dp, slot_index].set(
        out_cache[0].reshape(SAMP_DEV, ROWS, feature_width)
    )
    got_in, got_out = (
        lax.all_to_all(send_in, "dp", split_axis=0, concat_axis=0, tiled=True),
        lax.all_to_all(send_out, "dp", split_axis=0, concat_axis=0, tiled=True),
    )
    total_samples = sample_map.shape[0]
    inverse = (
        jnp.zeros((total_samples,), jnp.int32)
        .at[sample_map]
        .set(jnp.arange(total_samples, dtype=jnp.int32))
    )
    own_sources = lax.dynamic_slice_in_dim(inverse, own_device * SAMP_DEV, SAMP_DEV)
    source_device = own_sources // SAMP_DEV
    source_dp = source_device // expert_count
    source_local = own_sources % SAMP_DEV
    source_maps = sample_map.reshape(group_size, SAMP_DEV)[source_device]
    goes_here = source_maps // SAMP_DEV // expert_count == own_dp
    earlier = sample_ids[None, :] < source_local[:, None]
    arrival_slot = jnp.sum((goes_here & earlier).astype(jnp.int32), axis=1)
    in_moved = got_in[source_dp, arrival_slot].reshape(tok_rows, feature_width)
    out_moved = got_out[source_dp, arrival_slot].reshape(tok_rows, feature_width)
    tokens = inputs[0]
    flat_experts = routing[0].reshape(-1)
    sorted_order = jnp.argsort(flat_experts, stable=True)
    per_expert = tok_rows * TOPK // EXPERTS
    grouped = tokens[sorted_order // TOPK].reshape(EXPERTS, 1, per_expert, feature_width)
    outgoing = jnp.broadcast_to(grouped, (EXPERTS, slice_count, per_expert, feature_width)).reshape(
        group_size, per_expert, feature_width
    )
    up_slice = w_up[0]
    down_slice = w_down[0]
    arrived = lax.all_to_all(outgoing, ("dp", "expert"), split_axis=0, concat_axis=0, tiled=True)
    flat_rows = arrived.reshape(-1, feature_width)
    hidden = jax.nn.silu(jnp.dot(flat_rows, up_slice, preferred_element_type=jnp.float32)).astype(
        jnp.bfloat16
    )
    partial_value = jnp.dot(hidden, down_slice, preferred_element_type=jnp.float32).astype(
        jnp.bfloat16
    )
    returned = lax.all_to_all(
        partial_value.reshape(arrived.shape),
        ("dp", "expert"),
        split_axis=0,
        concat_axis=0,
        tiled=True,
    )
    summed = jnp.sum(
        returned.astype(jnp.float32).reshape(EXPERTS, slice_count, per_expert, feature_width),
        axis=1,
    )
    summed = summed.reshape(-1, feature_width)
    position = (
        jnp.zeros_like(sorted_order)
        .at[sorted_order]
        .set(jnp.arange(sorted_order.shape[0], dtype=jnp.int32))
    )
    per_assign = summed[position].reshape(tok_rows, TOPK, feature_width)
    weights = gate_table[0].astype(jnp.float32)
    weights = weights / jnp.sum(weights, axis=1, keepdims=True)
    mixed = jnp.sum(weights[:, :, None] * per_assign, axis=1)
    row_numbers = jnp.arange(tok_rows, dtype=jnp.int32) % ROWS
    valid_rows = row_numbers < jnp.repeat(lengths, ROWS)
    delta_rows = jnp.where(
        valid_rows[:, None],
        (mixed - out_moved.astype(jnp.float32)).astype(jnp.bfloat16),
        jnp.zeros((), jnp.bfloat16),
    )
    new_out = (out_moved.astype(jnp.float32) + delta_rows.astype(jnp.float32)).astype(jnp.bfloat16)
    received = from_behind(delta_rows, "section", 1)
    next_input = (in_moved.astype(jnp.float32) + received.astype(jnp.float32)).astype(jnp.bfloat16)
    return (next_input[None], new_out[None])


def solution(mesh):
    placed = (
        P("section", ("dp", "expert"), None),
        P("section", ("dp", "expert"), None),
        P("section", ("dp", "expert"), None),
        P("section", None, ("dp", "expert")),
        P("section", ("dp", "expert"), None),
        P("section", ("dp", "expert"), None),
        P("section", ("dp", "expert"), None),
        P(("dp", "expert")),
        P(),
    )
    return jax.shard_map(
        per_device,
        mesh=mesh,
        in_specs=placed,
        out_specs=(P("section", ("dp", "expert"), None), P("section", ("dp", "expert"), None)),
        check_vma=False,
    )
```

profile of v0, /device:TPU:1, one launch (start us, length us, event | category | flops | bytes accessed | tf_op | source)
XLA Modules:
  0.0 129.2 jit_solution(5529909485898635782)
XLA Ops:
  0.6 0.0 copy-start
  0.6 0.0 copy-start.5
  0.7 0.0 copy-start.3
  0.7 0.9 copy.13
  1.5 0.1 reshape_squeeze.10
  1.7 3.2 %sort.17 = (s32[256]{0:T(256)}, s32[256]{0:T(256)S(1)}) sort(s32[256]{0:T(256)S(1)} %reshape_squeeze.10, s32[256]{0:T(256)S(1)} %iota.29), dimensions={0}, to_apply=%region_5.6 | sort | flops 2048 | bytes 4096 | tf_op jit(solution)/shard_map/jit(argsort)/sort | solution.py:64
  4.9 0.0 copy-done
  4.9 2.3 %gather_fusion.3 = bf16[256,2048]{1,0:T(8,128)(2,1)} fusion(bf16[128,2048]{1,0:T(8,128)(2,1)S(1)} %bitcast.81, s32[1024]{0:T(1024)S(1)} %pad_clamp_fusion.1), kind=kCustom, calls=%fused_computation.3 | custom fusion | bytes 2098176 | tf_op jit(solution)/shard_map/gather | solution.py:66
  7.2 6.3 %all-to-all-start.1 = ((bf16[8,32,2048]{2,1,0:T(8,128)(2,1)}), bf16[8,32,2048]{2,1,0:T(8,128)(2,1)S(1)}, u32[]{:S(2)}, u32[]{:S(2)}) async-start(bf16[8,32,2048]{2,1,0:T(8,128)(2,1)} %bitcast.11), calls=%async_computation.1 | async-start | bytes 2097152 | tf_op jit(solution)/shard_map/all_to_all | solution.py:72
  13.6 0.0 copy-done.5
  13.6 0.1 fusion.41
  13.7 0.1 fusion.24
  13.8 0.1 fusion.28
  13.9 0.6 gather_fusion
  14.5 0.8 broadcast_in_dim.62.clone
  15.4 0.0 copy-done.3
  15.4 2.5 %scatter_fusion.1 = bf16[2,4,16,2048]{3,2,1,0:T(8,128)(2,1)} fusion(bf16[2,4,16,2048]{3,2,1,0:T(8,128)(2,1)} %broadcast_in_dim.62.clone, s32[8]{0:T(128)S(1)} %fusion.43, bf16[8,16,2048]{2,1,0:T(8,128)(2,1)S(1)} %bitcast.84), kind=kCustom, calls=%fused_computation.9 | custom fusion | bytes 1572928 | tf_op jit(solution)/shard_map/scatter | solution.py:39
  17.9 21.2 %all-to-all-done.1 = bf16[8,32,2048]{2,1,0:T(8,128)(2,1)S(1)} async-done(((bf16[8,32,2048]{2,1,0:T(8,128)(2,1)}), bf16[8,32,2048]{2,1,0:T(8,128)(2,1)S(1)}, u32[]{:S(2)}, u32[]{:S(2)}) %all-to-all-start.1) | async-done | bytes 1048608 | tf_op jit(solution)/shard_map/all_to_all | solution.py:72
  39.1 3.5 %all-to-all-start.3 = ((bf16[2,4,16,2048]{3,2,1,0:T(8,128)(2,1)}), bf16[2,4,16,2048]{3,2,1,0:T(8,128)(2,1)S(1)}, u32[]{:S(2)}, u32[]{:S(2)}) async-start(bf16[2,4,16,2048]{3,2,1,0:T(8,128)(2,1)} %scatter_fusion.1), calls=%async_computation.3 | async-start | bytes 1048576 | tf_op jit(solution)/shard_map/all_to_all | solution.py:44
  42.6 0.0 copy-start.6
  42.6 0.0 copy-start.7
  42.6 0.0 copy-start.4
  42.6 25.5 %fusion.9 = bf16[256,2048]{1,0:T(8,128)(2,1)} fusion(bf16[1,7168,2048]{2,1,0:T(8,128)(2,1)} %param.13, bf16[256,2048]{1,0:T(8,128)(2,1)S(1)} %bitcast.83, bf16[1,2048,7168]{2,1,0:T(8,128)(2,1)} %param.12), kind=kOutput, calls=%fused_computation.16 | convolution fusion | flops 15042084864 | bytes 60817408 | tf_op jit(solution)/shard_map/dot_general | solution.py:77
  68.1 0.0 all-to-all-done.3
  68.1 3.6 %all-to-all-start.2 = ((bf16[8,32,2048]{2,1,0:T(8,128)(2,1)}), bf16[8,32,2048]{2,1,0:T(8,128)(2,1)S(1)}, u32[]{:S(2)}, u32[]{:S(2)}) async-start(bf16[8,32,2048]{2,1,0:T(8,128)(2,1)} %bitcast.15), calls=%async_computation.2 | async-start | bytes 2097152 | tf_op jit(solution)/shard_map/all_to_all | solution.py:80
  71.6 0.0 copy-done.6
  71.7 0.1 reshape.152
  71.7 0.1 copy.12
  71.9 0.0 copy-done.7
  71.9 0.1 broadcast_in_dim.67
  71.9 0.1 reshape.153
  72.0 1.4 %scatter_custom_fusion.2 = s32[256]{0:T(256)S(1)} fusion(s32[256]{0:T(256)S(1)} %get-tuple-element.10, s32[256]{0:T(256)S(1)} %iota.30, s32[]{:T(128)} %constant.117.clone.1), kind=kCustom, calls=%fused_computation.100 | custom fusion | bytes 1028 | tf_op jit(solution)/shard_map/scatter | solution.py:95
  73.5 0.8 scatter_custom_fusion.1
  74.2 0.1 and_select_fusion.2
  74.3 0.1 compare_select_fusion.7
  74.4 0.6 gather_fusion.1
  75.0 0.8 broadcast_in_dim.62.clone.1
  75.8 0.0 copy-done.4
  75.8 2.5 %scatter_fusion = bf16[2,4,16,2048]{3,2,1,0:T(8,128)(2,1)} fusion(bf16[2,4,16,2048]{3,2,1,0:T(8,128)(2,1)} %broadcast_in_dim.62.clone.1, s32[8]{0:T(128)S(1)} %fusion.43, bf16[8,16,2048]{2,1,0:T(8,128)(2,1)S(1)} %bitcast.85), kind=kCustom, calls=%fused_computation.6 | custom fusion | bytes 1572928 | tf_op jit(solution)/shard_map/scatter | solution.py:36
  78.3 0.2 convert_reduce_fusion
  78.5 0.6 gather_fusion.5
  79.1 16.7 %all-to-all-done.2 = bf16[8,32,2048]{2,1,0:T(8,128)(2,1)S(1)} async-done(((bf16[8,32,2048]{2,1,0:T(8,128)(2,1)}), bf16[8,32,2048]{2,1,0:T(8,128)(2,1)S(1)}, u32[]{:S(2)}, u32[]{:S(2)}) %all-to-all-start.2) | async-done | bytes 1048608 | tf_op jit(solution)/shard_map/all_to_all | solution.py:80
  95.9 0.0 copy-start.2
  95.9 1.0 copy-done.2
  96.9 4.4 %all-to-all-start = ((bf16[2,4,16,2048]{3,2,1,0:T(8,128)(2,1)}), bf16[2,4,16,2048]{3,2,1,0:T(8,128)(2,1)}, u32[]{:S(2)}, u32[]{:S(2)}) async-start(bf16[2,4,16,2048]{3,2,1,0:T(8,128)(2,1)} %scatter_fusion), calls=%async_computation | async-start | bytes 1048576 | tf_op jit(solution)/shard_map/all_to_all | solution.py:43
  101.3 1.5 %bitcast_convert_fusion = f32[256,2048]{1,0:T(8,128)S(1)} fusion(bf16[8,32,2048]{2,1,0:T(8,128)(2,1)} %copy-done.2), kind=kLoop, calls=%fused_computation.18 | loop fusion | flops 524288 | bytes 3145728 | tf_op jit(solution)/shard_map/reshape | solution.py:91
  102.7 0.0 copy-start.1
  102.7 2.7 %gather_fusion.4 = f32[256,2048]{1,0:T(8,128)} fusion(f32[256,2048]{1,0:T(8,128)S(1)} %bitcast_convert_fusion, s32[1024]{0:T(1024)S(1)} %pad_clamp_fusion), kind=kCustom, calls=%fused_computation.4 | custom fusion | bytes 4195328 | tf_op jit(solution)/shard_map/gather | solution.py:97
  105.4 3.5 %reshape.158 = f32[128,2,2048]{2,1,0:T(2,128)} reshape(f32[256,2048]{1,0:T(8,128)} %gather_fusion.4) | data formatting | bytes 4194304 | tf_op jit(solution)/shard_map/reshape | solution.py:97
  108.9 4.7 %multiply_reduce_fusion = f32[128,2048]{1,0:T(8,128)S(1)} fusion(f32[128,2,2048]{2,1,0:T(2,128)} %reshape.158, f32[128,2]{1,0:T(8,128)S(1)} %copy.12), kind=kLoop, calls=%fused_computation.17 | loop fusion | flops 786432 | bytes 3146752 | tf_op jit(solution)/shard_map/reduce_sum | solution.py:100
  113.6 0.9 fusion.18
  114.6 6.3 %collective-permute-start = (bf16[128,2048]{1,0:T(8,128)(2,1)}, bf16[128,2048]{1,0:T(8,128)(2,1)}, u32[]{:S(2)}, u32[]{:S(2)}) collective-permute-start(bf16[128,2048]{1,0:T(8,128)(2,1)} %fusion.18), channel_id=1, source_target_pairs={{0,8},{8,16},{16,24},{1,9},{9,17},{17,25},{2,10},{10,18},{18,26},{... | collective-permute-start | bytes 1572872 | tf_op jit(solution)/shard_map/ppermute | solution.py:15
  120.9 0.1 convert_element_type.105
  121.0 0.0 all-to-all-done
  121.0 1.6 %gather_fusion.2 = bf16[8,16,2048]{2,1,0:T(8,128)(2,1)S(1)} fusion(bf16[2,4,16,2048]{3,2,1,0:T(8,128)(2,1)} %all-to-all-done, s32[8]{0:T(128)S(1)} %fusion.42), kind=kCustom, calls=%fused_computation.2 | custom fusion | bytes 1048640 | tf_op jit(solution)/shard_map/gather | solution.py:60
  122.6 1.1 fusion.16
  123.7 3.6 %collective-permute-done = bf16[128,2048]{1,0:T(8,128)(2,1)} collective-permute-done((bf16[128,2048]{1,0:T(8,128)(2,1)}, bf16[128,2048]{1,0:T(8,128)(2,1)}, u32[]{:S(2)}, u32[]{:S(2)}) %collective-permute-start) | collective-permute-done | bytes 524320 | tf_op jit(solution)/shard_map/ppermute | solution.py:15
  127.3 2.0 %fusion.20 = bf16[1,128,2048]{2,1,0:T(8,128)(2,1)} fusion(bf16[128,2048]{1,0:T(8,128)(2,1)} %collective-permute-done, bf16[8,16,2048]{2,1,0:T(8,128)(2,1)S(1)} %gather_fusion.2), kind=kLoop, calls=%fused_computation.29 | loop fusion | flops 1048576 | bytes 1572864 | tf_op jit(solution)/shard_map/broadcast_in_dim | solution.py:111
  129.2 0.0 copy-done.1
  (15 shorter events, 0.1 us)
Async XLA Ops:
  0.6 4.3 %copy-start = (bf16[1,128,2048]{2,1,0:T(8,128)(2,1)S(1)}, bf16[1,128,2048]{2,1,0:T(8,128)(2,1)}, u32[]{:S(2)}) copy-start(bf16[1,128,2048]{2,1,0:T(8,128)(2,1)} %param.9) | copy-start | bytes 1572868
  0.6 12.9 %copy-start.5 = (s32[64]{0:T(128)S(1)}, s32[64]{0:T(128)}, u32[]{:S(2)}) copy-start(s32[64]{0:T(128)} %param.17) | copy-start | bytes 772
  0.7 14.7 %copy-start.3 = (bf16[1,128,2048]{2,1,0:T(8,128)(2,1)S(1)}, bf16[1,128,2048]{2,1,0:T(8,128)(2,1)}, u32[]{:S(2)}) copy-start(bf16[1,128,2048]{2,1,0:T(8,128)(2,1)} %param.11) | copy-start | bytes 1572868
  7.2 31.8 %all-to-all-start.1 = ((bf16[8,32,2048]{2,1,0:T(8,128)(2,1)}), bf16[8,32,2048]{2,1,0:T(8,128)(2,1)S(1)}, u32[]{:S(2)}, u32[]{:S(2)}) async-start(bf16[8,32,2048]{2,1,0:T(8,128)(2,1)} %bitcast.11), calls=%async_computation.1 | async-start | bytes 2097152 | tf_op jit(solution)/shard_map/all_to_all | solution.py:72
  39.1 29.0 %all-to-all-start.3 = ((bf16[2,4,16,2048]{3,2,1,0:T(8,128)(2,1)}), bf16[2,4,16,2048]{3,2,1,0:T(8,128)(2,1)S(1)}, u32[]{:S(2)}, u32[]{:S(2)}) async-start(bf16[2,4,16,2048]{3,2,1,0:T(8,128)(2,1)} %scatter_fusion.1), calls=%async_computation.3 | async-start | bytes 1048576 | tf_op jit(solution)/shard_map/all_to_all | solution.py:44
  42.6 29.1 %copy-start.6 = (s32[1,128,2]{1,2,0:T(2,128)S(1)}, s32[1,128,2]{1,2,0:T(2,128)}, u32[]{:S(2)}) copy-start(s32[1,128,2]{1,2,0:T(2,128)} %param.15) | copy-start | bytes 3076
  42.6 29.3 %copy-start.7 = (s32[8]{0:T(128)S(1)}, s32[8]{0:T(128)}, u32[]{:S(2)}) copy-start(s32[8]{0:T(128)} %param.16) | copy-start | bytes 100
  42.6 33.2 %copy-start.4 = (bf16[1,128,2048]{2,1,0:T(8,128)(2,1)S(1)}, bf16[1,128,2048]{2,1,0:T(8,128)(2,1)}, u32[]{:S(2)}) copy-start(bf16[1,128,2048]{2,1,0:T(8,128)(2,1)} %param.10) | copy-start | bytes 1572868
  68.1 27.8 %all-to-all-start.2 = ((bf16[8,32,2048]{2,1,0:T(8,128)(2,1)}), bf16[8,32,2048]{2,1,0:T(8,128)(2,1)S(1)}, u32[]{:S(2)}, u32[]{:S(2)}) async-start(bf16[8,32,2048]{2,1,0:T(8,128)(2,1)} %bitcast.15), calls=%async_computation.2 | async-start | bytes 2097152 | tf_op jit(solution)/shard_map/all_to_all | solution.py:80
  95.9 1.0 copy-start.2
  96.9 24.1 %all-to-all-start = ((bf16[2,4,16,2048]{3,2,1,0:T(8,128)(2,1)}), bf16[2,4,16,2048]{3,2,1,0:T(8,128)(2,1)}, u32[]{:S(2)}, u32[]{:S(2)}) async-start(bf16[2,4,16,2048]{3,2,1,0:T(8,128)(2,1)} %scatter_fusion), calls=%async_computation | async-start | bytes 1048576 | tf_op jit(solution)/shard_map/all_to_all | solution.py:43
  102.7 26.5 %copy-start.1 = (bf16[1,128,2048]{2,1,0:T(8,128)(2,1)S(1)}, bf16[1,128,2048]{2,1,0:T(8,128)(2,1)}, u32[]{:S(2)}) copy-start(bf16[1,128,2048]{2,1,0:T(8,128)(2,1)} %param.9) | copy-start | bytes 1572868
  114.6 12.7 %collective-permute-start = (bf16[128,2048]{1,0:T(8,128)(2,1)}, bf16[128,2048]{1,0:T(8,128)(2,1)}, u32[]{:S(2)}, u32[]{:S(2)}) collective-permute-start(bf16[128,2048]{1,0:T(8,128)(2,1)} %fusion.18), channel_id=1, source_target_pairs={{0,8},{8,16},{16,24},{1,9},{9,17},{17,25},{2,10},{10,18},{18,26},{... | collective-permute-start | bytes 1572872 | tf_op jit(solution)/shard_map/ppermute | solution.py:15
where the time goes:
time: 130 us; the launch traced here: 129 us
  waiting for transfers between devices  41.5 us (32%)
  matrix products  25.5 us (20%)
  starting transfers between devices  24 us (18%)
  local copies, waits for them, and re-layouts  23.2 us (18%)
  other arithmetic  14.2 us (11%)
    dot_general x1, matrix products, per_device(): jnp.dot(hidden, down_slice, preferred_element_type=jnp.float32)  25.5 us
    all_to_all x1, waiting for transfers between devices, per_device(): lax.all_to_all(outgoing, ('dp', 'expert'), split_axis=0, concat_axis=0, t...  21.2 us
    all_to_all x1, waiting for transfers between devices, per_device(): lax.all_to_all(partial_value.reshape(arrived.shape), ('dp', 'expert'), sp...  16.7 us
    all_to_all x1, starting transfers between devices, per_device(): lax.all_to_all(outgoing, ('dp', 'expert'), split_axis=0, concat_axis=0, t...  6.34 us
    ppermute x1, starting transfers between devices, from_behind(): return lax.ppermute(value, axis, pairs)  6.28 us
    scatter x2, local copies, waits for them, and re-layouts, per_device(): empty_slots.at[dest_dp, slot_index]  5 us
    reduce_sum x1, other arithmetic, per_device(): mixed = jnp.sum(weights[:, :, None] * per_assign, axis=1)  4.74 us
    all_to_all x1, starting transfers between devices, per_device(): lax.all_to_all(send_in, 'dp', split_axis=0, concat_axis=0, tiled=True)  4.38 us
  transfers between devices with their start and end apart: 5, of which 3 were waited for; matrix products, arithmetic and copies ran while one was open for 41% of the time, Pallas kernels for 0%

commit v1 on v0

v1 whole, which is shorter than its diff:
```python
import jax
import jax.numpy as jnp
from jax import lax
from jax.sharding import PartitionSpec as P

EXPERTS = 8
TOPK = 2
ROWS = 16
SAMP_DEV = 8


def from_behind(value, axis, by):
    peers = lax.axis_size(axis)
    pairs = [(i, i + by) for i in range(peers) if 0 <= i + by < peers]
    return lax.ppermute(value, axis, pairs)


def cache_plan(sample_map, own_device, own_dp, dp_count, expert_count, cap_slots):
    total = sample_map.shape[0]
    ids = jnp.arange(total, dtype=jnp.int32)
    local = jnp.arange(SAMP_DEV, dtype=jnp.int32)
    own_map = lax.dynamic_slice_in_dim(sample_map, own_device * SAMP_DEV, SAMP_DEV)
    dest_dp = own_map // (SAMP_DEV * expert_count)
    slot = jnp.sum(
        ((dest_dp[:, None] == dest_dp[None, :]) & (local[None, :] < local[:, None])).astype(jnp.int32),
        axis=1,
    )
    places = jnp.arange(dp_count * cap_slots, dtype=jnp.int32)
    to_send = jnp.sum(
        jnp.where(places[:, None] == (dest_dp * cap_slots + slot)[None, :], local[None, :], 0), axis=1
    )
    wanted = own_device * SAMP_DEV + local
    sources = jnp.sum(jnp.where(sample_map[None, :] == wanted[:, None], ids[None, :], 0), axis=1)
    source_device = sources // SAMP_DEV
    earlier = (
        (ids[None, :] // SAMP_DEV == source_device[:, None])
        & (ids[None, :] < sources[:, None])
        & (sample_map[None, :] // (SAMP_DEV * expert_count) == own_dp)
    )
    arrival = source_device // expert_count * cap_slots + jnp.sum(earlier.astype(jnp.int32), axis=1)
    return to_send, arrival


def token_plan(routing, gate_table, per_expert):
    tok_rows = routing.shape[0]
    before = jnp.arange(tok_rows)[None, :] < jnp.arange(tok_rows)[:, None]
    weights = gate_table.astype(jnp.float32)
    weights = weights / jnp.sum(weights, axis=1, keepdims=True)
    slots = jnp.arange(EXPERTS * per_expert, dtype=jnp.int32)
    select, mix = 0, 0
    for k in range(TOPK):
        own = routing[:, k]
        rank = 0
        for j in range(TOPK):
            rank = rank + jnp.sum((before & (routing[:, j][None, :] == own[:, None])).astype(jnp.int32), axis=1)
        slot = own * per_expert + rank
        select = select + (slots[:, None] == slot[None, :]).astype(jnp.bfloat16)
        mix = mix + jnp.where(slots[None, :] == slot[:, None], weights[:, k][:, None], 0.0)
    return select, mix


def per_device(inputs, in_cache, out_cache, w_up, w_down, routing, gate_table, lengths, sample_map):
    tok_rows, width = inputs.shape[1:]
    dp_count = lax.axis_size("dp")
    expert_count = lax.axis_size("expert")
    group_size = dp_count * expert_count
    slice_count = group_size // EXPERTS
    own_dp = lax.axis_index("dp")
    own_device = own_dp * expert_count + lax.axis_index("expert")
    cap_slots = max(1, SAMP_DEV // dp_count)
    per_expert = tok_rows * TOPK // EXPERTS

    select, mix = token_plan(routing[0], gate_table[0], per_expert)
    grouped = jnp.dot(select, inputs[0], preferred_element_type=jnp.float32).astype(jnp.bfloat16)
    grouped = grouped.reshape(EXPERTS, 1, per_expert, width)
    outgoing = jnp.broadcast_to(grouped, (EXPERTS, slice_count, per_expert, width)).reshape(
        group_size, per_expert, width
    )
    arrived = lax.all_to_all(outgoing, ("dp", "expert"), split_axis=0, concat_axis=0, tiled=True)

    to_send, arrival = cache_plan(sample_map, own_device, own_dp, dp_count, expert_count, cap_slots)
    send = jnp.concatenate(
        [
            in_cache[0].reshape(SAMP_DEV, 1, ROWS, width)[to_send],
            out_cache[0].reshape(SAMP_DEV, 1, ROWS, width)[to_send],
        ],
        axis=1,
    )
    send, arrived = lax.optimization_barrier((send, arrived))
    got = lax.all_to_all(send, "dp", split_axis=0, concat_axis=0, tiled=True)

    hidden = jax.nn.silu(
        jnp.dot(arrived.reshape(-1, width), w_up[0], preferred_element_type=jnp.float32)
    ).astype(jnp.bfloat16)
    partial_value = jnp.dot(hidden, w_down[0], preferred_element_type=jnp.float32).astype(jnp.bfloat16)
    returned = lax.all_to_all(
        partial_value.reshape(arrived.shape), ("dp", "expert"), split_axis=0, concat_axis=0, tiled=True
    ).reshape(-1, width)

    mix = jnp.broadcast_to(
        mix.reshape(tok_rows, EXPERTS, 1, per_expert), (tok_rows, EXPERTS, slice_count, per_expert)
    ).reshape(tok_rows, -1)
    high = mix.astype(jnp.bfloat16)
    low = (mix - high.astype(jnp.float32)).astype(jnp.bfloat16)
    both = jnp.dot(jnp.concatenate([high, low], axis=0), returned, preferred_element_type=jnp.float32)
    mixed = both[:tok_rows] + both[tok_rows:]

    in_moved = got[arrival, 0].reshape(tok_rows, width)
    out_moved = got[arrival, 1].reshape(tok_rows, width)
    row_numbers = jnp.arange(tok_rows, dtype=jnp.int32) % ROWS
    valid_rows = row_numbers < jnp.repeat(lengths, ROWS)
    delta_rows = jnp.where(
        valid_rows[:, None],
        (mixed - out_moved.astype(jnp.float32)).astype(jnp.bfloat16),
        jnp.zeros((), jnp.bfloat16),
    )
    new_out = (out_moved.astype(jnp.float32) + delta_rows.astype(jnp.float32)).astype(jnp.bfloat16)
    received = from_behind(delta_rows, "section", 1)
    next_input = (in_moved.astype(jnp.float32) + received.astype(jnp.float32)).astype(jnp.bfloat16)
    return (next_input[None], new_out[None])


def solution(mesh):
    split = P("section", ("dp", "expert"), None)
    placed = (split, split, split, P("section", None, ("dp", "expert")), split, split, split, P(("dp", "expert")), P())
    return jax.shard_map(per_device, mesh=mesh, in_specs=placed, out_specs=(split, split), check_vma=False)
```

time: 130 us -> 109 us (0.84)
  local copies, waits for them, and re-layouts: 23.2 us -> 5.37 us
  other arithmetic: 14.2 us -> 8.1 us
  waiting for transfers between devices: 41.5 us -> 46.7 us
  starting transfers between devices: 24 us -> 19.8 us
  matrix products: 25.5 us -> 27.4 us
    scatter x4 -> x0, local copies, waits for them, and re-layouts: 7.17 us -> none  [the longest x2 5 us: per_device(): empty_slots.at[dest_dp, slot_index]]
    all_to_all x1, waiting for transfers between devices: 16.7 us -> 22.9 us  [per_device(): lax.all_to_all(partial_value.reshape(arrived.shape), ('dp', 'expert'), sp...]
    all_to_all x2 -> x1, starting transfers between devices: 7.87 us -> 3.58 us  [per_device(): got = lax.all_to_all(send, 'dp', split_axis=0, concat_axis=0, tiled=True)]
    gather x6 -> x4, local copies, waits for them, and re-layouts: 8.45 us -> 4.41 us  [the longest x1 1.62 us: per_device(): out_cache[0].reshape(SAMP_DEV, 1, ROWS, width)[to_send]]
    reshape x2 -> x0, local copies, waits for them, and re-layouts: 3.53 us -> none  [the longest x1 3.46 us: per_device(): per_assign = summed[position].reshape(tok_rows, TOPK, feature_width)]
    reduce_sum x3 -> x6, other arithmetic: 4.94 us -> 1.58 us  [the longest x1 0.7 us: token_plan(): weights = weights / jnp.sum(weights, axis=1, keepdims=True)]
    all_to_all x1, waiting for transfers between devices: 21.2 us -> 18 us  [per_device(): lax.all_to_all(outgoing, ('dp', 'expert'), split_axis=0, concat_axis=0, t...]
    sort x1 -> x0, other arithmetic: 3.17 us -> none  [per_device(): sorted_order = jnp.argsort(flat_experts, stable=True)]
  transfers between devices with their start and end apart: 5 -> 4, of which waited for: 3 -> 3; matrix products, arithmetic and copies ran while one was open for 41% -> 32% of each run, Pallas kernels for 0% -> 0%
where the time goes in v1:
time: 109 us; the launch traced here: 108 us
  waiting for transfers between devices  46.7 us (43%)
  matrix products  27.4 us (25%)
  starting transfers between devices  19.8 us (18%)
  other arithmetic  8.1 us (7%)
  local copies, waits for them, and re-layouts  5.37 us (5%)
    dot_general x1, matrix products, per_device(): jnp.dot(hidden, w_down[0], preferred_element_type=jnp.float32)  25.5 us
    all_to_all x1, waiting for transfers between devices, per_device(): lax.all_to_all(partial_value.reshape(arrived.shape), ('dp', 'expert'), sp...  22.9 us
    all_to_all x1, waiting for transfers between devices, per_device(): lax.all_to_all(outgoing, ('dp', 'expert'), split_axis=0, concat_axis=0, t...  18 us
    all_to_all x1, starting transfers between devices, per_device(): lax.all_to_all(outgoing, ('dp', 'expert'), split_axis=0, concat_axis=0, t...  6.34 us
    ppermute x1, starting transfers between devices, from_behind(): return lax.ppermute(value, axis, pairs)  6.27 us
    ppermute x1, waiting for transfers between devices, from_behind(): return lax.ppermute(value, axis, pairs)  5.83 us
    all_to_all x1, starting transfers between devices, per_device(): got = lax.all_to_all(send, 'dp', split_axis=0, concat_axis=0, tiled=True)  3.58 us
    all_to_all x1, starting transfers between devices, per_device(): lax.all_to_all(partial_value.reshape(arrived.shape), ('dp', 'expert'), sp...  3.56 us
  transfers between devices with their start and end apart: 4, of which 3 were waited for; matrix products, arithmetic and copies ran while one was open for 32% of the time, Pallas kernels for 0%

profile of v1, /device:TPU:1, one launch (start us, length us, event | category | flops | bytes accessed | tf_op | source)
XLA Modules:
  0.0 108.1 jit_solution(17019754017804990186)
XLA Ops:
  0.6 0.0 copy-start
  0.6 0.8 slice_bitcast_fusion.3
  1.4 0.2 convert_reduce_fusion.2
  1.6 0.8 multiply_add_fusion.1
  2.4 0.0 copy-done
  2.4 1.5 %convolution_convert_fusion = bf16[256,2048]{1,0:T(8,128)(2,1)} fusion(bf16[1,128,2048]{2,1,0:T(8,128)(2,1)S(1)} %copy-done, s32[128]{0:T(128)S(1)} %get-tuple-element.21, s32[128]{0:T(128)S(1)} %get-tuple-element.20), kind=kOutput, calls=%fused_computation.10 | convolution fusion | flops 135004160 | bytes 1573888 | tf_op jit(solution)/shard_map/dot_general | solution.py:74
  3.8 6.3 %all-to-all-start = ((bf16[8,32,2048]{2,1,0:T(8,128)(2,1)}), bf16[8,32,2048]{2,1,0:T(8,128)(2,1)S(1)}, u32[]{:S(2)}, u32[]{:S(2)}) async-start(bf16[8,32,2048]{2,1,0:T(8,128)(2,1)} %bitcast.10), calls=%async_computation | async-start | bytes 2097152 | tf_op jit(solution)/shard_map/all_to_all | solution.py:79
  10.2 0.7 and_select_fusion.6
  10.9 0.2 convert_reduce_fusion.5
  11.1 0.7 multiply_add_fusion.2
  11.9 0.1 select_reduce_fusion.1
  12.0 1.6 %gather_fusion.1 = bf16[8,16,2048]{2,1,0:T(8,128)(2,1)S(1)} fusion(bf16[8,16,2048]{2,1,0:T(8,128)(2,1)} %bitcast.101, s32[1024]{0:T(1024)S(1)} %pad_clamp_fusion), kind=kCustom, calls=%fused_computation.1 | custom fusion | bytes 1048608 | tf_op jit(solution)/shard_map/gather | solution.py:85
  13.6 1.6 %gather_fusion = bf16[8,16,2048]{2,1,0:T(8,128)(2,1)S(1)} fusion(bf16[8,16,2048]{2,1,0:T(8,128)(2,1)} %bitcast.102, s32[1024]{0:T(1024)S(1)} %pad_clamp_fusion), kind=kCustom, calls=%fused_computation | custom fusion | bytes 1048608 | tf_op jit(solution)/shard_map/gather | solution.py:84
  15.3 0.7 convert_reduce_fusion.6
  16.0 0.7 fusion.46
  16.6 1.1 %pad_maximum_fusion = bf16[8,2,16,2048]{3,2,1,0:T(8,128)(2,1)} fusion(bf16[8,1,16,2048]{3,2,1,0:T(8,128)(2,1)S(1)} %bitcast.97, bf16[8,1,16,2048]{3,2,1,0:T(8,128)(2,1)S(1)} %bitcast.98), kind=kLoop, calls=%fused_computation.17 | loop fusion | flops 524288 | bytes 2097152 | tf_op jit(solution)/shard_map/concatenate | solution.py:82
  17.7 18.0 %all-to-all-done = bf16[8,32,2048]{2,1,0:T(8,128)(2,1)S(1)} async-done(((bf16[8,32,2048]{2,1,0:T(8,128)(2,1)}), bf16[8,32,2048]{2,1,0:T(8,128)(2,1)S(1)}, u32[]{:S(2)}, u32[]{:S(2)}) %all-to-all-start) | async-done | bytes 1048608 | tf_op jit(solution)/shard_map/all_to_all | solution.py:79
  35.7 3.6 %all-to-all-start.1 = ((bf16[8,2,16,2048]{3,2,1,0:T(8,128)(2,1)}), bf16[8,2,16,2048]{3,2,1,0:T(8,128)(2,1)S(1)}, u32[]{:S(2)}, u32[]{:S(2)}) async-start(bf16[8,2,16,2048]{3,2,1,0:T(8,128)(2,1)} %pad_maximum_fusion), calls=%async_computation.1 | async-start | bytes 2097152 | tf_op jit(solution)/shard_map/all_to_all | solution.py:90
  39.3 0.0 copy-start.4
  39.3 0.0 copy-start.5
  39.3 0.0 copy-start.3
  39.3 0.0 copy-start.2
  39.3 0.0 copy-start.1
  39.3 25.5 %fusion.9 = bf16[256,2048]{1,0:T(8,128)(2,1)} fusion(bf16[1,7168,2048]{2,1,0:T(8,128)(2,1)} %param.13, bf16[256,2048]{1,0:T(8,128)(2,1)S(1)} %bitcast.99, bf16[1,2048,7168]{2,1,0:T(8,128)(2,1)} %param.12), kind=kOutput, calls=%fused_computation.11 | convolution fusion | flops 15042084864 | bytes 60817408 | tf_op jit(solution)/shard_map/dot_general | solution.py:95
  64.8 0.0 all-to-all-done.1
  64.8 3.6 %all-to-all-start.2 = ((bf16[8,32,2048]{2,1,0:T(8,128)(2,1)}), bf16[8,32,2048]{2,1,0:T(8,128)(2,1)S(1)}, u32[]{:S(2)}, u32[]{:S(2)}) async-start(bf16[8,32,2048]{2,1,0:T(8,128)(2,1)} %bitcast.100), calls=%async_computation.2 | async-start | bytes 2097152 | tf_op jit(solution)/shard_map/all_to_all | solution.py:96
  68.4 0.0 copy-done.4
  68.4 0.1 broadcast_in_dim.102
  68.5 0.1 reshape.280
  68.6 0.0 copy-done.5
  68.6 0.2 select_reduce_fusion
  68.8 0.2 convert_reduce_fusion.4
  69.0 0.0 copy-done.3
  69.0 0.0 copy-done.2
  69.1 0.1 fusion.25
  69.2 0.6 gather_fusion.3
  69.8 22.9 %all-to-all-done.2 = bf16[8,32,2048]{2,1,0:T(8,128)(2,1)S(1)} async-done(((bf16[8,32,2048]{2,1,0:T(8,128)(2,1)}), bf16[8,32,2048]{2,1,0:T(8,128)(2,1)S(1)}, u32[]{:S(2)}, u32[]{:S(2)}) %all-to-all-start.2) | async-done | bytes 1048608 | tf_op jit(solution)/shard_map/all_to_all | solution.py:96
  92.7 0.4 fusion.21
  93.1 1.4 %fusion.18 = (bf16[1,128,2048]{2,1,0:T(8,128)(2,1)}, bf16[128,2048]{1,0:T(8,128)(2,1)}) fusion(bf16[8,16,2048]{2,1,0:T(8,128)(2,1)S(1)} %gather_fusion.3, f32[256,2048]{1,0:T(8,128)S(1)} %fusion.21, pred[128]{0:T(512)(128)(4,1)S(1)} %fusion.40), kind=kLoop, calls=%fused_computation.21 | loop fusion | flops 2097152 | bytes 3670144 | tf_op jit(solution)/shard_map/broadcast_in_dim | solution.py:120
  94.5 6.3 %collective-permute-start = (bf16[128,2048]{1,0:T(8,128)(2,1)}, bf16[128,2048]{1,0:T(8,128)(2,1)S(1)}, u32[]{:S(2)}, u32[]{:S(2)}) collective-permute-start(bf16[128,2048]{1,0:T(8,128)(2,1)} %get-tuple-element.11), channel_id=1, source_target_pairs={{0,8},{8,16},{16,24},{1,9},{9,17},{17,25},{2,10},{10,18},{18,26},{... | collective-permute-start | bytes 1572872 | tf_op jit(solution)/shard_map/ppermute | solution.py:15
  100.7 0.6 gather_fusion.2
  101.3 5.8 %collective-permute-done = bf16[128,2048]{1,0:T(8,128)(2,1)S(1)} collective-permute-done((bf16[128,2048]{1,0:T(8,128)(2,1)}, bf16[128,2048]{1,0:T(8,128)(2,1)S(1)}, u32[]{:S(2)}, u32[]{:S(2)}) %collective-permute-start) | collective-permute-done | bytes 524320 | tf_op jit(solution)/shard_map/ppermute | solution.py:15
  107.2 1.0 fusion.17
  108.1 0.0 copy-done.1
  (10 shorter events, 0.1 us)
Async XLA Ops:
  0.6 1.8 %copy-start = (bf16[1,128,2048]{2,1,0:T(8,128)(2,1)S(1)}, bf16[1,128,2048]{2,1,0:T(8,128)(2,1)}, u32[]{:S(2)}) copy-start(bf16[1,128,2048]{2,1,0:T(8,128)(2,1)} %param.9) | copy-start | bytes 1572868
  3.8 31.8 %all-to-all-start = ((bf16[8,32,2048]{2,1,0:T(8,128)(2,1)}), bf16[8,32,2048]{2,1,0:T(8,128)(2,1)S(1)}, u32[]{:S(2)}, u32[]{:S(2)}) async-start(bf16[8,32,2048]{2,1,0:T(8,128)(2,1)} %bitcast.10), calls=%async_computation | async-start | bytes 2097152 | tf_op jit(solution)/shard_map/all_to_all | solution.py:79
  35.7 29.2 %all-to-all-start.1 = ((bf16[8,2,16,2048]{3,2,1,0:T(8,128)(2,1)}), bf16[8,2,16,2048]{3,2,1,0:T(8,128)(2,1)S(1)}, u32[]{:S(2)}, u32[]{:S(2)}) async-start(bf16[8,2,16,2048]{3,2,1,0:T(8,128)(2,1)} %pad_maximum_fusion), calls=%async_computation.1 | async-start | bytes 2097152 | tf_op jit(solution)/shard_map/all_to_all | solution.py:90
  39.3 29.2 %copy-start.4 = (s32[8]{0:T(128)S(1)}, s32[8]{0:T(128)}, u32[]{:S(2)}) copy-start(s32[8]{0:T(128)} %param.16) | copy-start | bytes 100
  39.3 29.3 %copy-start.5 = (s32[64]{0:T(128)S(1)}, s32[64]{0:T(128)}, u32[]{:S(2)}) copy-start(s32[64]{0:T(128)} %param.17) | copy-start | bytes 772
  39.3 29.7 %copy-start.3 = (s32[1,128,2]{1,2,0:T(2,128)S(1)}, s32[1,128,2]{1,2,0:T(2,128)}, u32[]{:S(2)}) copy-start(s32[1,128,2]{1,2,0:T(2,128)} %param.15) | copy-start | bytes 3076
  39.3 29.7 %copy-start.2 = (s32[1,128,2]{1,2,0:T(2,128)S(1)}, s32[1,128,2]{1,2,0:T(2,128)}, u32[]{:S(2)}) copy-start(s32[1,128,2]{1,2,0:T(2,128)} %param.14) | copy-start | bytes 3076
  39.3 68.8 %copy-start.1 = (bf16[1,128,2048]{2,1,0:T(8,128)(2,1)S(1)}, bf16[1,128,2048]{2,1,0:T(8,128)(2,1)}, u32[]{:S(2)}) copy-start(bf16[1,128,2048]{2,1,0:T(8,128)(2,1)} %param.9) | copy-start | bytes 1572868
  64.8 27.8 %all-to-all-start.2 = ((bf16[8,32,2048]{2,1,0:T(8,128)(2,1)}), bf16[8,32,2048]{2,1,0:T(8,128)(2,1)S(1)}, u32[]{:S(2)}, u32[]{:S(2)}) async-start(bf16[8,32,2048]{2,1,0:T(8,128)(2,1)} %bitcast.100), calls=%async_computation.2 | async-start | bytes 2097152 | tf_op jit(solution)/shard_map/all_to_all | solution.py:96
  94.5 12.7 %collective-permute-start = (bf16[128,2048]{1,0:T(8,128)(2,1)}, bf16[128,2048]{1,0:T(8,128)(2,1)S(1)}, u32[]{:S(2)}, u32[]{:S(2)}) collective-permute-start(bf16[128,2048]{1,0:T(8,128)(2,1)} %get-tuple-element.11), channel_id=1, source_target_pairs={{0,8},{8,16},{16,24},{1,9},{9,17},{17,25},{2,10},{10,18},{18,26},{... | collective-permute-start | bytes 1572872 | tf_op jit(solution)/shard_map/ppermute | solution.py:15

commit v2 on v1

--- a/solution.py
+++ b/solution.py
@@ -1,6 +1,10 @@
+import functools
+
 import jax
 import jax.numpy as jnp
 from jax import lax
+from jax.experimental import pallas as pl
+from jax.experimental.pallas import tpu as pltpu
 from jax.sharding import PartitionSpec as P
 
 EXPERTS = 8
@@ -59,6 +63,202 @@
     return select, mix
 
 
+BLOCK = 512
+DOWN_SLOTS = 2
+KERNEL_VMEM = 62 * 1024 * 1024
+
+
+def section_kernel(
+    dp_count, expert_count, per_expert,
+    grouped, mix, in_cache, out_cache, w_up, w_down, mixed, other,
+    up_buf, down_buf, arrived, hidden, part, returned,
+    up_sem, down_sem, own_sem, there_send, there_recv, back_send, back_recv, back_own, cache_send, cache_recv,
+):
+    own_dp, own_expert = lax.axis_index("dp"), lax.axis_index("expert")
+    me = own_dp * expert_count + own_expert
+    tok_rows = mixed.shape[0]
+    ups, downs = w_up.shape[1] // BLOCK, w_down.shape[1] // BLOCK
+
+    def up_copy(f):
+        columns = pl.ds(pl.multiple_of(f * BLOCK, BLOCK), BLOCK)
+        return pltpu.make_async_copy(w_up.at[:, columns], up_buf.at[f], up_sem.at[f])
+
+    def down_copy(n):
+        columns = pl.ds(n * BLOCK, BLOCK)
+        return pltpu.make_async_copy(w_down.at[:, columns], down_buf.at[n % DOWN_SLOTS], down_sem.at[n])
+
+    half = expert_count // 2
+    steps = sorted(
+        ((de, dd) for de in range(expert_count) for dd in range(dp_count) if de or dd),
+        key=lambda step: (abs(step[0] - half), step[1]),
+    )
+
+    def partner(de, dd):
+        return lax.rem(own_dp + dd, dp_count), lax.rem(own_expert + de, expert_count)
+
+    def rows_of(device):
+        return pl.ds(pl.multiple_of(device * per_expert, per_expert), per_expert)
+
+    barrier = pltpu.get_barrier_semaphore()
+    for de, dd in steps:
+        dp, expert = partner(de, dd)
+        pl.semaphore_signal(
+            barrier, inc=1, device_id={"dp": dp, "expert": expert}, device_id_type=pl.DeviceIdType.MESH
+        )
+    own_there = pltpu.make_async_copy(grouped.at[rows_of(me)], arrived.at[rows_of(me)], own_sem)
+    own_there.start()
+    pl.semaphore_wait(barrier, len(steps))
+
+    sends = []
+    for i, (de, dd) in enumerate(steps):
+        dp, expert = partner(de, dd)
+        sends.append(
+            pltpu.make_async_remote_copy(
+                src_ref=grouped.at[rows_of(dp * expert_count + expert)],
+                dst_ref=arrived.at[rows_of(me)],
+                send_sem=there_send.at[i],
+                recv_sem=there_recv.at[i],
+                device_id={"dp": dp, "expert": expert},
+                device_id_type=pl.DeviceIdType.MESH,
+            )
+        )
+        sends[-1].start()
+    cache_copies = []
+    for dd in range(1, dp_count):
+        for c, cache in enumerate((out_cache, in_cache)):
+            cache_copies.append(
+                pltpu.make_async_remote_copy(
+                    src_ref=cache,
+                    dst_ref=other.at[dd - 1, c],
+                    send_sem=cache_send.at[dd - 1, c],
+                    recv_sem=cache_recv.at[dd - 1, c],
+                    device_id={"dp": lax.rem(own_dp + dd, dp_count)},
+                    device_id_type=pl.DeviceIdType.MESH,
+                )
+            )
+            cache_copies[-1].start()
+
+    @pl.loop(0, ups)
+    def _(f):
+        up_copy(f).start()
+
+    for n in range(min(DOWN_SLOTS, downs)):
+        down_copy(n).start()
+
+    own_there.wait()
+    for copy in sends:
+        copy.wait()
+
+    @pl.loop(0, ups)
+    def _(f):
+        up_copy(f).wait()
+        value = jnp.dot(arrived[...], up_buf[f], preferred_element_type=jnp.float32)
+        columns = pl.ds(pl.multiple_of(f * BLOCK, BLOCK), BLOCK)
+        hidden[:, columns] = (value / (1.0 + jnp.exp(-value))).astype(jnp.bfloat16)
+
+    backs = []
+    for n in range(downs):
+        columns = pl.ds(n * BLOCK, BLOCK)
+        down_copy(n).wait()
+        value = jnp.dot(hidden[...], down_buf[n % DOWN_SLOTS], preferred_element_type=jnp.float32)
+        part[:, columns] = value.astype(jnp.bfloat16)
+        if n + DOWN_SLOTS < downs:
+            down_copy(n + DOWN_SLOTS).start()
+        group = []
+        for i, (de, dd) in enumerate(steps):
+            dp, expert = partner(de, dd)
+            group.append(
+                pltpu.make_async_remote_copy(
+                    src_ref=part.at[rows_of(dp * expert_count + expert), columns],
+                    dst_ref=returned.at[rows_of(me), columns],
+                    send_sem=back_send.at[n, i],
+                    recv_sem=back_recv.at[n, i],
+                    device_id={"dp": dp, "expert": expert},
+                    device_id_type=pl.DeviceIdType.MESH,
+                )
+            )
+            group[-1].start()
+        group.append(
+            pltpu.make_async_copy(part.at[rows_of(me), columns], returned.at[rows_of(me), columns], back_own.at[n])
+        )
+        group[-1].start()
+        backs.append(group)
+
+    for n in range(downs):
+        columns = pl.ds(n * BLOCK, BLOCK)
+        for copy in backs[n]:
+            copy.wait()
+        both = jnp.dot(mix[...], returned[:, columns], preferred_element_type=jnp.float32)
+        mixed[:, columns] = both[:tok_rows] + both[tok_rows:]
+    for copy in cache_copies:
+        copy.wait()
+
+
+def run_section_kernel(grouped, mix, in_cache, out_cache, w_up, w_down, per_expert):
+    dp_count, expert_count = lax.axis_size("dp"), lax.axis_size("expert")
+    tok_rows, width = in_cache.shape
+    slots, units = grouped.shape[0], w_up.shape[1]
+    peers = dp_count * expert_count - 1
+    ups, downs = units // BLOCK, width // BLOCK
+    vmem, anywhere = pl.BlockSpec(memory_space=pltpu.VMEM), pl.BlockSpec(memory_space=pl.ANY)
+    dma = pltpu.SemaphoreType.DMA
+    return pl.pallas_call(
+        functools.partial(section_kernel, dp_count, expert_count, per_expert),
+        out_shape=(
+            jax.ShapeDtypeStruct((tok_rows, width), jnp.float32),
+            jax.ShapeDtypeStruct((dp_count - 1, 2, tok_rows, width), jnp.bfloat16),
+        ),
+        in_specs=[vmem, vmem, anywhere, anywhere, anywhere, anywhere],
+        out_specs=(vmem, anywhere),
+        scratch_shapes=[
+            pltpu.VMEM((ups, width, BLOCK), jnp.bfloat16),
+            pltpu.VMEM((DOWN_SLOTS, units, BLOCK), jnp.bfloat16),
+            pltpu.VMEM((slots, width), jnp.bfloat16),
+            pltpu.VMEM((slots, units), jnp.bfloat16),
+            pltpu.VMEM((slots, width), jnp.bfloat16),
+            pltpu.VMEM((slots, width), jnp.bfloat16),
+            dma((ups,)),
+            dma((downs,)),
+            dma,
+            dma((peers,)),
+            dma((peers,)),
+            dma((downs, peers)),
+            dma((downs, peers)),
+            dma((downs,)),
+            dma((dp_count - 1, 2)),
+            dma((dp_count - 1, 2)),
+        ],
+        compiler_params=pltpu.CompilerParams(
+            collective_id=0, has_side_effects=True, vmem_limit_bytes=KERNEL_VMEM
+        ),
+        cost_estimate=pl.CostEstimate(
+            flops=4 * slots * width * units, bytes_accessed=4 * width * units, transcendentals=slots * units
+        ),
+    )(grouped, mix, in_cache, out_cache, w_up, w_down)
+
+
+def fits_kernel(tok_rows, width, units, dp_count, group_size):
+    slots = tok_rows * TOPK
+    needed = 2 * (width * units + DOWN_SLOTS * units * BLOCK + slots * units + 8 * slots * width)
+    whole = units % BLOCK == 0 and width % BLOCK == 0
+    return group_size == EXPERTS and dp_count == 2 and whole and needed < KERNEL_VMEM
+
+
+def own_part(sample_map, own_device, expert_count, tok_rows):
+    dp_count = lax.axis_size("dp")
+    ids = jnp.arange(sample_map.shape[0], dtype=jnp.int32)
+    wanted = own_device * SAMP_DEV + jnp.arange(SAMP_DEV, dtype=jnp.int32)
+    sources = jnp.sum(jnp.where(sample_map[None, :] == wanted[:, None], ids[None, :], 0), axis=1)
+    back = lax.rem(lax.axis_index("dp") - sources // (SAMP_DEV * expert_count) + dp_count, dp_count)
+    rows = jnp.arange(tok_rows, dtype=jnp.int32)
+    row_source = jnp.repeat(sources % SAMP_DEV, ROWS) * ROWS + rows % ROWS
+    row_back = jnp.repeat(back, ROWS)
+    return [
+        ((row_source[:, None] == rows[None, :]) & (row_back[:, None] == away)).astype(jnp.bfloat16)
+        for away in range(dp_count)
+    ]
+
+
 def per_device(inputs, in_cache, out_cache, w_up, w_down, routing, gate_table, lengths, sample_map):
     tok_rows, width = inputs.shape[1:]
     dp_count = lax.axis_size("dp")
@@ -72,41 +272,58 @@
 
     select, mix = token_plan(routing[0], gate_table[0], per_expert)
     grouped = jnp.dot(select, inputs[0], preferred_element_type=jnp.float32).astype(jnp.bfloat16)
-    grouped = grouped.reshape(EXPERTS, 1, per_expert, width)
-    outgoing = jnp.broadcast_to(grouped, (EXPERTS, slice_count, per_expert, width)).reshape(
-        group_size, per_expert, width
-    )
-    arrived = lax.all_to_all(outgoing, ("dp", "expert"), split_axis=0, concat_axis=0, tiled=True)
-
-    to_send, arrival = cache_plan(sample_map, own_device, own_dp, dp_count, expert_count, cap_slots)
-    send = jnp.concatenate(
-        [
-            in_cache[0].reshape(SAMP_DEV, 1, ROWS, width)[to_send],
-            out_cache[0].reshape(SAMP_DEV, 1, ROWS, width)[to_send],
-        ],
-        axis=1,
-    )
-    send, arrived = lax.optimization_barrier((send, arrived))
-    got = lax.all_to_all(send, "dp", split_axis=0, concat_axis=0, tiled=True)
-
-    hidden = jax.nn.silu(
-        jnp.dot(arrived.reshape(-1, width), w_up[0], preferred_element_type=jnp.float32)
-    ).astype(jnp.bfloat16)
-    partial_value = jnp.dot(hidden, w_down[0], preferred_element_type=jnp.float32).astype(jnp.bfloat16)
-    returned = lax.all_to_all(
-        partial_value.reshape(arrived.shape), ("dp", "expert"), split_axis=0, concat_axis=0, tiled=True
-    ).reshape(-1, width)
-
-    mix = jnp.broadcast_to(
-        mix.reshape(tok_rows, EXPERTS, 1, per_expert), (tok_rows, EXPERTS, slice_count, per_expert)
-    ).reshape(tok_rows, -1)
-    high = mix.astype(jnp.bfloat16)
-    low = (mix - high.astype(jnp.float32)).astype(jnp.bfloat16)
-    both = jnp.dot(jnp.concatenate([high, low], axis=0), returned, preferred_element_type=jnp.float32)
-    mixed = both[:tok_rows] + both[tok_rows:]
-
-    in_moved = got[arrival, 0].reshape(tok_rows, width)
-    out_moved = got[arrival, 1].reshape(tok_rows, width)
+    if fits_kernel(tok_rows, width, w_up.shape[2], dp_count, group_size):
+        high = mix.astype(jnp.bfloat16)
+        low = (mix - high.astype(jnp.float32)).astype(jnp.bfloat16)
+        mixed, other = run_section_kernel(
+            grouped, jnp.concatenate([high, low], axis=0), in_cache[0], out_cache[0], w_up[0], w_down[0], per_expert
+        )
+        picks = own_part(sample_map, own_device, expert_count, tok_rows)
+
+        def moved(own, c):
+            total = jnp.dot(picks[0], own, preferred_element_type=jnp.float32)
+            for away in range(1, dp_count):
+                total = total + jnp.dot(picks[away], other[away - 1, c], preferred_element_type=jnp.float32)
+            return total.astype(jnp.bfloat16)
+
+        out_moved, in_moved = moved(out_cache[0], 0), moved(in_cache[0], 1)
+    else:
+        grouped = grouped.reshape(EXPERTS, 1, per_expert, width)
+        outgoing = jnp.broadcast_to(grouped, (EXPERTS, slice_count, per_expert, width)).reshape(
+            group_size, per_expert, width
+        )
+        arrived = lax.all_to_all(outgoing, ("dp", "expert"), split_axis=0, concat_axis=0, tiled=True)
+
+        to_send, arrival = cache_plan(sample_map, own_device, own_dp, dp_count, expert_count, cap_slots)
+        send = jnp.concatenate(
+            [
+                in_cache[0].reshape(SAMP_DEV, 1, ROWS, width)[to_send],
+                out_cache[0].reshape(SAMP_DEV, 1, ROWS, width)[to_send],
+            ],
+            axis=1,
+        )
+        send, arrived = lax.optimization_barrier((send, arrived))
+        got = lax.all_to_all(send, "dp", split_axis=0, concat_axis=0, tiled=True)
+
+        hidden = jax.nn.silu(
+            jnp.dot(arrived.reshape(-1, width), w_up[0], preferred_element_type=jnp.float32)
+        ).astype(jnp.bfloat16)
+        partial_value = jnp.dot(hidden, w_down[0], preferred_element_type=jnp.float32).astype(jnp.bfloat16)
+        returned = lax.all_to_all(
+            partial_value.reshape(arrived.shape), ("dp", "expert"), split_axis=0, concat_axis=0, tiled=True
+        ).reshape(-1, width)
+
+        mix = jnp.broadcast_to(
+            mix.reshape(tok_rows, EXPERTS, 1, per_expert), (tok_rows, EXPERTS, slice_count, per_expert)
+        ).reshape(tok_rows, -1)
+        high = mix.astype(jnp.bfloat16)
+        low = (mix - high.astype(jnp.float32)).astype(jnp.bfloat16)
+        both = jnp.dot(jnp.concatenate([high, low], axis=0), returned, preferred_element_type=jnp.float32)
+        mixed = both[:tok_rows] + both[tok_rows:]
+
+        in_moved = got[arrival, 0].reshape(tok_rows, width)
+        out_moved = got[arrival, 1].reshape(tok_rows, width)
+
     row_numbers = jnp.arange(tok_rows, dtype=jnp.int32) % ROWS
     valid_rows = row_numbers < jnp.repeat(lengths, ROWS)
     delta_rows = jnp.where(

time: 109 us -> 91.7 us (0.84)
  Pallas kernels: 0 us -> 64.7 us
  waiting for transfers between devices: 46.7 us -> 4.71 us
  matrix products: 27.4 us -> 8.94 us
  starting transfers between devices: 19.8 us -> 5.25 us
  local copies, waits for them, and re-layouts: 5.37 us -> 2.06 us
  other arithmetic: 8.1 us -> 4.88 us
    pallas_call x0 -> x1, Pallas kernels: none -> 64.7 us  [run_section_kernel(): pl.pallas_call(functools.partial(section_kernel, dp_count, expert_count,...]
    all_to_all x3 -> x0, waiting for transfers between devices: 40.8 us -> none  [the longest x1 22.9 us: per_device(): lax.all_to_all(partial_value.reshape(arrived.shape), ('dp', 'expert'), sp...]
    dot_general x2 -> x4, matrix products: 26 us -> 7.53 us  [the longest x2 4.76 us: moved(): jnp.dot(picks[away], other[away - 1, c], preferred_element_type=jnp.float32)]
    all_to_all x3 -> x0, starting transfers between devices: 13.5 us -> none  [the longest x1 6.34 us: per_device(): lax.all_to_all(outgoing, ('dp', 'expert'), split_axis=0, concat_axis=0, t...]
    gather x4 -> x0, local copies, waits for them, and re-layouts: 4.41 us -> none  [the longest x1 1.62 us: per_device(): out_cache[0].reshape(SAMP_DEV, 1, ROWS, width)[to_send]]
    broadcast_in_dim x2 -> x0, other arithmetic: 2.31 us -> none  [per_device(): return (next_input[None], new_out[None])]
    ppermute x1, waiting for transfers between devices: 5.83 us -> 4.71 us  [from_behind(): return lax.ppermute(value, axis, pairs)]
  transfers between devices with their start and end apart: 4 -> 1, of which waited for: 3 -> 1; matrix products, arithmetic and copies ran while one was open for 32% -> 2% of each run, Pallas kernels for 0% -> 0%
where the time goes in v2:
time: 91.7 us; the launch traced here: 91.2 us
  Pallas kernels  64.7 us (71%)
  matrix products  8.94 us (10%)
  starting transfers between devices  5.25 us (6%)
  other arithmetic  4.88 us (5%)
  waiting for transfers between devices  4.71 us (5%)
  local copies, waits for them, and re-layouts  2.06 us (2%)
    pallas_call x1, Pallas kernels, run_section_kernel(): pl.pallas_call(functools.partial(section_kernel, dp_count, expert_count,...  64.7 us
    ppermute x1, starting transfers between devices, from_behind(): return lax.ppermute(value, axis, pairs)  5.25 us
    dot_general x2, matrix products, moved(): jnp.dot(picks[away], other[away - 1, c], preferred_element_type=jnp.float32)  4.76 us
    ppermute x1, waiting for transfers between devices, from_behind(): return lax.ppermute(value, axis, pairs)  4.71 us
    dot_general x2, matrix products, moved(): total = jnp.dot(picks[0], own, preferred_element_type=jnp.float32)  2.77 us
  transfers between devices with their start and end apart: 1, of which 1 were waited for; matrix products, arithmetic and copies ran while one was open for 2% of the time, Pallas kernels for 0%

profile of v2, /device:TPU:1, one launch (start us, length us, event | category | flops | bytes accessed | tf_op | source)
XLA Modules:
  0.0 91.2 jit_solution(4714549573240716507)
XLA Ops:
  0.6 0.0 copy-start
  0.7 0.9 select_reduce_fusion
  1.6 0.8 slice_bitcast_fusion.3
  2.3 0.2 convert_reduce_fusion.2
  2.6 0.8 fusion.44
  3.3 0.8 multiply_add_fusion.1
  4.1 0.1 broadcast_in_dim.86
  4.2 0.1 eq.183
  4.3 0.1 broadcast_in_dim.85
  4.3 0.1 eq.181
  4.4 0.7 convert_reduce_fusion.4
  5.1 0.7 bitcast_divide_fusion
  5.8 0.1 broadcast_in_dim.84
  5.9 0.1 mul.46
  6.0 0.7 broadcast_in_dim.92
  6.7 0.1 reshape.105
  6.8 0.1 fusion.14
  6.9 0.7 pad_maximum_fusion.mix
  7.6 0.0 copy-done
  7.6 1.4 %convolution_convert_fusion.grouped = bf16[256,2048]{1,0:T(8,128)(2,1)} fusion(bf16[1,128,2048]{2,1,0:T(8,128)(2,1)S(1)} %copy-done, s32[128]{0:T(128)S(1)} %get-tuple-element.21, s32[128]{0:T(128)S(1)} %get-tuple-element.20), kind=kOutput, calls=%fused_computation | convolution fusion | flops 135004160 | bytes 1573888 | tf_op jit(solution)/shard_map/dot_general | solution.py:274
  9.0 1.4 %fusion.28 = f32[128,2048]{1,0:T(8,128)S(1)} fusion(s32[128]{0:T(128)S(1)} %fusion.47, pred[128]{0:T(512)(128)(4,1)S(1)} %eq.181, bf16[1,128,2048]{2,1,0:T(8,128)(2,1)} %param.11), kind=kOutput, calls=%fused_computation.43 | convolution fusion | flops 67141632 | bytes 1573504 | tf_op jit(solution)/shard_map/dot_general | solution.py:284
  10.4 64.7 %shard_map.104 = (f32[128,2048]{1,0:T(8,128)}, bf16[1,2,128,2048]{3,2,1,0:T(8,128)(2,1)}) custom-call(bf16[256,2048]{1,0:T(8,128)(2,1)} %convolution_convert_fusion.grouped, bf16[256,256]{1,0:T(8,128)(2,1)} %pad_maximum_fusion.mix, bf16[128,2048]{1,0:T(8,128)(2,1)} %bitcast.55, bf16[128,2048]{1,0:T(8,128)(2,1)} %bitcast.54, bf16[2048,7168]{1,0:T(8,128)(2,1)} %bitcast.52, ...), custom_call_target="tpu_custom_call" | custom-call | flops 15032385536 | bytes 58720256 | tf_op jit(solution)/shard_map/pallas_call | solution.py:205
  75.1 2.6 %fusion.6 = (bf16[1,128,2048]{2,1,0:T(8,128)(2,1)}, bf16[128,2048]{1,0:T(8,128)(2,1)S(1)}) fusion(f32[128,2048]{1,0:T(8,128)} %get-tuple-element.5, pred[128]{0:T(512)(128)(4,1)S(1)} %fusion.46, f32[128,2048]{1,0:T(8,128)S(1)} %fusion.28, bf16[1,2,128,2048]{3,2,1,0:T(8,128)(2,1)} %get-tuple-element.4, s32[128]{0:T(128)S(1)} %fusion.47, ...), kind=kOutput, calls=%fused_computation.12 | convolution fusion | flops 69500928 | bytes 3670784 | tf_op jit(solution)/shard_map/dot_general | solution.py:286
  77.7 5.3 %collective-permute-start = (bf16[128,2048]{1,0:T(8,128)(2,1)S(1)}, bf16[128,2048]{1,0:T(8,128)(2,1)S(1)}, u32[]{:S(2)}, u32[]{:S(2)}) collective-permute-start(bf16[128,2048]{1,0:T(8,128)(2,1)S(1)} %get-tuple-element.11), channel_id=1, source_target_pairs={{0,8},{8,16},{16,24},{1,9},{9,17},{17,25},{2,10},{10,18},{18,26},{... | collective-permute-start | bytes 1572872 | tf_op jit(solution)/shard_map/ppermute | solution.py:19
  82.9 1.4 %fusion.30 = f32[128,2048]{1,0:T(8,128)S(1)} fusion(s32[128]{0:T(128)S(1)} %fusion.47, pred[128]{0:T(512)(128)(4,1)S(1)} %eq.181, bf16[1,128,2048]{2,1,0:T(8,128)(2,1)} %param.10), kind=kOutput, calls=%fused_computation.44 | convolution fusion | flops 67141632 | bytes 1573504 | tf_op jit(solution)/shard_map/dot_general | solution.py:284
  84.3 4.7 %collective-permute-done = bf16[128,2048]{1,0:T(8,128)(2,1)S(1)} collective-permute-done((bf16[128,2048]{1,0:T(8,128)(2,1)S(1)}, bf16[128,2048]{1,0:T(8,128)(2,1)S(1)}, u32[]{:S(2)}, u32[]{:S(2)}) %collective-permute-start) | collective-permute-done | bytes 524320 | tf_op jit(solution)/shard_map/ppermute | solution.py:19
  89.0 2.2 %fusion.5 = bf16[1,128,2048]{2,1,0:T(8,128)(2,1)} fusion(bf16[128,2048]{1,0:T(8,128)(2,1)S(1)} %collective-permute-done, f32[128,2048]{1,0:T(8,128)S(1)} %fusion.30, bf16[1,2,128,2048]{3,2,1,0:T(8,128)(2,1)} %get-tuple-element.4, s32[128]{0:T(128)S(1)} %fusion.47, pred[128]{0:T(512)(128)(4,1)S(1)} %eq.183), kind=kOutput, calls=%fused_computation.11 | convolution fusion | flops 68714496 | bytes 2622080 | tf_op jit(solution)/shard_map/dot_general | solution.py:286
  (7 shorter events, 0.1 us)
Async XLA Ops:
  0.6 7.0 %copy-start = (bf16[1,128,2048]{2,1,0:T(8,128)(2,1)S(1)}, bf16[1,128,2048]{2,1,0:T(8,128)(2,1)}, u32[]{:S(2)}) copy-start(bf16[1,128,2048]{2,1,0:T(8,128)(2,1)} %param.9) | copy-start | bytes 1572868
  77.7 11.4 %collective-permute-start = (bf16[128,2048]{1,0:T(8,128)(2,1)S(1)}, bf16[128,2048]{1,0:T(8,128)(2,1)S(1)}, u32[]{:S(2)}, u32[]{:S(2)}) collective-permute-start(bf16[128,2048]{1,0:T(8,128)(2,1)S(1)} %get-tuple-element.11), channel_id=1, source_target_pairs={{0,8},{8,16},{16,24},{1,9},{9,17},{17,25},{2,10},{10,18},{18,26},{... | collective-permute-start | bytes 1572872 | tf_op jit(solution)/shard_map/ppermute | solution.py:19
